TPU v7x, 32 devices: a whole 2x2x4 slice. The times are simulated.
32 devices in a mesh: groups: 2 (over x), sph: 16 (over z, y, core).
Axes of the slice: x: 2, y: 2, z: 4, core: 2. Of those that a mesh axis runs over, the one named last changes fastest.
Arguments:
- positions: float32 [512, 3], P('sph'), may hold values from -8 to 8
- wave_vectors: float32 [256, 3], replicated, may hold values from -5 to 5
- pattern: float32 [2, 448, 256], replicated, may hold values from -6 to 6
- dir_index: int32 [64], P('groups'), parts along dimension 0, may hold values from 0 to 255
- mie: float32 [2, 448, 512], P(None, None, 'sph'), may hold values from -0.9 to 0.9
- trans_table: bfloat16 [8, 2, 448, 448], replicated, may hold values from -0.1875 to 0.1875
- pair_route: int32 [1024, 1], P('sph'), may hold values from 0 to 15; in each aligned block of 64 rows (0 to 63, 64 to 127, ...) at most 8 rows name the same one
- pair_source: int32 [1024], P('sph'), may hold values from 0 to 15
- pair_target: int32 [1024], P('sph'), may hold values from 0 to 15
- pair_class: int32 [1024], P('sph'), may hold values from 0 to 7
Outputs:
- scattered: bfloat16 [896, 32768], P(None, ('groups', 'sph')), parts along dimension 1
- extinction: float32 [64], P('groups'), parts along dimension 0
There are 2 independent parts, one for each index of `groups`. A program takes and returns all parts, laid end to end along the dimension named above; an argument that names none is the same for every part. Nothing has to cross between parts.
Inputs may be any that keep to these rules, and one draw needn't show every extreme that they name: `pair_route`: among the rows of one device no device is named by more than 8 pairs, and in every draw some device is named by exactly 8 of them.
All inputs are finite; a program needn't handle non-finite values.
Results may differ from a plain program's by a relative error of at most 0.0051.
Values may be sent and summed in bfloat16 or wider, within the bound.
No kernel may reach another device: no remote copies, remote signals or barrier semaphores. Data moves between devices by JAX's collectives and lax.ppermute only.
A program may use at most 192 MiB of HBM per device.

v0:
```python
import jax
import jax.numpy as jnp
from jax import lax
from jax.sharding import PartitionSpec as P

BLOCK = 2


HIGHEST_PRECISION = lax.Precision.HIGHEST


def incident_field(positions, wave_vectors, pattern, dir_index):
    table_rows = wave_vectors.shape[0]
    select = (jnp.arange(table_rows, dtype=jnp.int32)[:, None] == dir_index[None, :]).astype(
        jnp.float32
    )
    directions = jnp.dot(select.T, wave_vectors, precision=HIGHEST_PRECISION)
    phases = (
        positions[:, 0:1] * directions[None, :, 0]
        + positions[:, 1:2] * directions[None, :, 1]
        + positions[:, 2:3] * directions[None, :, 2]
    )
    cosine = jnp.cos(phases)
    sine_part = jnp.sin(phases)
    chosen = jnp.einsum("cmt,td->cmd", pattern, select, precision=HIGHEST_PRECISION)
    inc_real = cosine[None] * chosen[0][:, None, :] - sine_part[None] * chosen[1][:, None, :]
    inc_imag = cosine[None] * chosen[1][:, None, :] + sine_part[None] * chosen[0][:, None, :]
    return (inc_real, inc_imag)


def translate(trans_table, classes, block_values):
    item_count = classes.shape[0]
    mode_count = trans_table.shape[2]
    grouped_classes = classes.reshape(item_count // 8, 8)
    grouped_values = block_values.reshape((item_count // 8, 8) + block_values.shape[1:])

    def one_group(group_items):
        picked, values = group_items
        tables = trans_table[picked]
        data_real = values[:, :mode_count]
        data_imag = values[:, mode_count:]
        part_real = jnp.einsum(
            "kij,kjc->kic", tables[:, 0], data_real, preferred_element_type=jnp.float32
        ) - jnp.einsum("kij,kjc->kic", tables[:, 1], data_imag, preferred_element_type=jnp.float32)
        part_imag = jnp.einsum(
            "kij,kjc->kic", tables[:, 1], data_real, preferred_element_type=jnp.float32
        ) + jnp.einsum("kij,kjc->kic", tables[:, 0], data_imag, preferred_element_type=jnp.float32)
        return jnp.concatenate([part_real, part_imag], 1).astype(jnp.bfloat16)

    return lax.map(one_group, (grouped_classes, grouped_values)).reshape(block_values.shape)


def shards(
    positions,
    wave_vectors,
    pattern,
    dir_index,
    mie,
    trans_table,
    pair_route,
    pair_source,
    pair_target,
    pair_class,
):
    mode_count = pattern.shape[1]
    spheres = positions.shape[0]
    directions = dir_index.shape[0]
    columns = BLOCK * directions
    block_count = spheres // BLOCK
    devices = lax.axis_size("sph")
    pair_count = pair_source.shape[0]
    capacity = max(2, 2 * pair_count // devices)
    slot_count = devices * capacity
    inc_real, inc_imag = incident_field(positions, wave_vectors, pattern, dir_index)
    mie_real = mie[0][:, :, None]
    mie_imag = mie[1][:, :, None]
    scat_real = mie_real * inc_real - mie_imag * inc_imag
    scat_imag = mie_real * inc_imag + mie_imag * inc_real
    coeffs = jnp.concatenate([scat_real, scat_imag], 0).astype(jnp.bfloat16)
    block_data = coeffs.reshape(2 * mode_count, block_count, columns).transpose(1, 0, 2)
    dest_device = pair_route[:, 0]
    by_device = (dest_device[:, None] == jnp.arange(devices, dtype=jnp.int32)[None, :]).astype(
        jnp.int32
    )
    before = jnp.cumsum(by_device, axis=0) - by_device
    rank_in = jnp.sum(before * by_device, axis=1)
    slot_of = dest_device * capacity + rank_in
    slot_match = (jnp.arange(slot_count, dtype=jnp.int32)[:, None] == slot_of[None, :]).astype(
        jnp.int32
    )
    filled = jnp.sum(slot_match, axis=1)
    slot_pair = jnp.sum(slot_match * jnp.arange(pair_count, dtype=jnp.int32)[None, :], axis=1)
    slot_target = jnp.where(filled > 0, pair_target[slot_pair], -1)
    keep_slot = filled.astype(jnp.bfloat16)[:, None, None]
    computed = translate(trans_table, pair_class, block_data[pair_source])
    outgoing = computed[slot_pair] * keep_slot
    outgoing = outgoing.reshape(devices, capacity, 2 * mode_count, columns)
    arrived = lax.all_to_all(outgoing, "sph", split_axis=0, concat_axis=0, tiled=True)
    targets = lax.all_to_all(
        slot_target.reshape(devices, capacity), "sph", split_axis=0, concat_axis=0, tiled=True
    ).reshape(slot_count)
    partial_value = arrived.reshape(slot_count, 2 * mode_count, columns)
    gather_matrix = (jnp.arange(block_count, dtype=jnp.int32)[:, None] == targets[None, :]).astype(
        jnp.bfloat16
    )
    summed = jnp.dot(
        gather_matrix,
        partial_value.reshape(slot_count, 2 * mode_count * columns),
        preferred_element_type=jnp.float32,
    )
    summed = (
        summed.reshape(block_count, 2 * mode_count, columns)
        .transpose(1, 0, 2)
        .reshape(2 * mode_count, spheres, directions)
    )
    total_real = inc_real + summed[:mode_count]
    total_imag = inc_imag + summed[mode_count:]
    out_real = mie_real * total_real - mie_imag * total_imag
    out_imag = mie_real * total_imag + mie_imag * total_real
    scattered = (
        jnp.concatenate([out_real, out_imag], 0)
        .reshape(2 * mode_count, spheres * directions)
        .astype(jnp.bfloat16)
    )
    local_ext = jnp.sum(inc_real * out_real + inc_imag * out_imag, axis=(0, 1))
    extinction = lax.psum(local_ext, "sph")
    return (scattered, extinction)


def solution(mesh):
    placed = (
        P("sph", None),
        P(),
        P(),
        P("groups"),
        P(None, None, "sph"),
        P(),
        P("sph", None),
        P("sph"),
        P("sph"),
        P("sph"),
    )
    return jax.shard_map(
        shards,
        mesh=mesh,
        in_specs=placed,
        out_specs=(P(None, ("groups", "sph")), P("groups")),
        check_vma=False,
    )
```

profile of v0, /device:TPU:0, one launch (start us, length us, event | category | flops | bytes accessed | tf_op | source)
XLA Modules:
  0.0 671.2 jit_solution(2450275542576880069)
XLA Ops:
  3.2 1.6 gather_fusion.1
  5.5 7.4 %all-to-all-start = ((s32[16,1,8]{2,1,0:T(1,128)}), s32[16,1,8]{2,1,0:T(1,128)S(1)}, u32[]{:S(2)}, u32[]{:S(2)}) async-start(s32[16,1,8]{2,1,0:T(1,128)} %bitcast.24), calls=%async_computation | async-start | bytes 16384 | tf_op jit(solution)/shard_map/all_to_all | solution.py:99
  21.9 4.3 gather_fusion.2
  26.3 134.5 %while.10 = (s32[]{:T(128)}, bf16[8,8,896,64]{2,3,1,0:T(8,128)(2,1)}, s32[8,8]{1,0:T(8,128)S(1)}, bf16[8,2,448,448]{3,2,1,0:T(8,128)(2,1)}, bf16[8,8,896,64]{2,3,1,0:T(8,128)(2,1)}, /*index=5*/s32[]{:T(128)}) while((s32[]{:T(128)}, bf16[8,8,896,64]{2,3,1,0:T(8,128)(2,1)}, s32[8,8]{1,0:T(8,128)S(1)}, bf16[8,2,448,448]{3,2,1,0:T(8,128)(2,1)}, ...), condition=%wide.region_5.6_spmd, body=%wide.region_4.5_spmd.sunk | while | flops 824837120 | bytes 63836904 | solution.py:50
  26.3 7.0 %gather_fusion = bf16[8,2,448,448]{3,2,1,0:T(8,128)(2,1)} fusion(bf16[8,2,448,448]{3,2,1,0:T(8,128)(2,1)} %get-tuple-element.133, s32[1024]{0:T(1024)S(1)} %pad_clamp_fusion.4), kind=kCustom, calls=%fused_computation.clone.1 | custom fusion | bytes 12845088 | tf_op jit(solution)/shard_map/while/body/eval_jaxpr/gather | solution.py:39
  34.7 3.5 fusion.68
  43.1 7.0 %gather_fusion = bf16[8,2,448,448]{3,2,1,0:T(8,128)(2,1)} fusion(bf16[8,2,448,448]{3,2,1,0:T(8,128)(2,1)} %get-tuple-element.133, s32[1024]{0:T(1024)S(1)} %pad_clamp_fusion.4), kind=kCustom, calls=%fused_computation.clone.1 | custom fusion | bytes 12845088 | tf_op jit(solution)/shard_map/while/body/eval_jaxpr/gather | solution.py:39
  51.5 3.5 fusion.68
  59.9 7.0 %gather_fusion = bf16[8,2,448,448]{3,2,1,0:T(8,128)(2,1)} fusion(bf16[8,2,448,448]{3,2,1,0:T(8,128)(2,1)} %get-tuple-element.133, s32[1024]{0:T(1024)S(1)} %pad_clamp_fusion.4), kind=kCustom, calls=%fused_computation.clone.1 | custom fusion | bytes 12845088 | tf_op jit(solution)/shard_map/while/body/eval_jaxpr/gather | solution.py:39
  68.3 3.5 fusion.68
  76.7 7.0 %gather_fusion = bf16[8,2,448,448]{3,2,1,0:T(8,128)(2,1)} fusion(bf16[8,2,448,448]{3,2,1,0:T(8,128)(2,1)} %get-tuple-element.133, s32[1024]{0:T(1024)S(1)} %pad_clamp_fusion.4), kind=kCustom, calls=%fused_computation.clone.1 | custom fusion | bytes 12845088 | tf_op jit(solution)/shard_map/while/body/eval_jaxpr/gather | solution.py:39
  85.1 3.5 fusion.68
  93.5 7.0 %gather_fusion = bf16[8,2,448,448]{3,2,1,0:T(8,128)(2,1)} fusion(bf16[8,2,448,448]{3,2,1,0:T(8,128)(2,1)} %get-tuple-element.133, s32[1024]{0:T(1024)S(1)} %pad_clamp_fusion.4), kind=kCustom, calls=%fused_computation.clone.1 | custom fusion | bytes 12845088 | tf_op jit(solution)/shard_map/while/body/eval_jaxpr/gather | solution.py:39
  101.9 3.5 fusion.68
  110.3 7.0 %gather_fusion = bf16[8,2,448,448]{3,2,1,0:T(8,128)(2,1)} fusion(bf16[8,2,448,448]{3,2,1,0:T(8,128)(2,1)} %get-tuple-element.133, s32[1024]{0:T(1024)S(1)} %pad_clamp_fusion.4), kind=kCustom, calls=%fused_computation.clone.1 | custom fusion | bytes 12845088 | tf_op jit(solution)/shard_map/while/body/eval_jaxpr/gather | solution.py:39
  118.7 3.5 fusion.68
  127.1 7.0 %gather_fusion = bf16[8,2,448,448]{3,2,1,0:T(8,128)(2,1)} fusion(bf16[8,2,448,448]{3,2,1,0:T(8,128)(2,1)} %get-tuple-element.133, s32[1024]{0:T(1024)S(1)} %pad_clamp_fusion.4), kind=kCustom, calls=%fused_computation.clone.1 | custom fusion | bytes 12845088 | tf_op jit(solution)/shard_map/while/body/eval_jaxpr/gather | solution.py:39
  135.5 3.4 fusion.68
  144.0 7.0 %gather_fusion = bf16[8,2,448,448]{3,2,1,0:T(8,128)(2,1)} fusion(bf16[8,2,448,448]{3,2,1,0:T(8,128)(2,1)} %get-tuple-element.133, s32[1024]{0:T(1024)S(1)} %pad_clamp_fusion.4), kind=kCustom, calls=%fused_computation.clone.1 | custom fusion | bytes 12845088 | tf_op jit(solution)/shard_map/while/body/eval_jaxpr/gather | solution.py:39
  152.4 3.5 fusion.68
  160.7 12.3 %gather_fusion.3 = bf16[128,896,64]{1,2,0:T(8,128)(2,1)} fusion(bf16[64,896,64]{1,2,0:T(8,128)(2,1)} %bitcast.33, s32[1024]{0:T(1024)S(1)} %pad_clamp_fusion.2), kind=kCustom, calls=%fused_computation.3 | custom fusion | bytes 29360640 | tf_op jit(solution)/shard_map/gather | solution.py:96
  173.1 13.5 %broadcast_multiply_fusion = bf16[16,8,896,64]{2,3,1,0:T(8,128)(2,1)} fusion(bf16[16,8,896,64]{2,3,1,0:T(8,128)(2,1)} %bitcast.236, bf16[16,8]{1,0:T(8,128)(2,1)S(1)} %convert_element_type.32), kind=kLoop, calls=%fused_computation.29 | loop fusion | flops 7340032 | bytes 29360384 | tf_op jit(solution)/shard_map/mul | solution.py:96
  186.6 6.1 all-to-all-start.1
  194.7 258.1 %all-to-all-done.1 = bf16[16,8,896,64]{2,3,1,0:T(8,128)(2,1)} async-done(((bf16[16,8,896,64]{2,3,1,0:T(8,128)(2,1)}), bf16[16,8,896,64]{2,3,1,0:T(8,128)(2,1)}, u32[]{:S(2)}, u32[]{:S(2)}) %all-to-all-start.1) | async-done | bytes 14680096 | tf_op jit(solution)/shard_map/all_to_all | solution.py:98
  452.8 26.5 %copy.80 = bf16[16,8,896,64]{3,2,1,0:T(8,128)(2,1)} copy(bf16[16,8,896,64]{2,3,1,0:T(8,128)(2,1)} %all-to-all-done.1) | data formatting | bytes 29360128 | tf_op jit(solution)/shard_map/all_to_all | solution.py:98
  479.3 28.1 %reshape_reshape.3 = bf16[128,57344]{1,0:T(8,128)(2,1)} reshape(bf16[16,8,896,64]{3,2,1,0:T(8,128)(2,1)} %copy.80) | data formatting | bytes 29360128 | tf_op jit(solution)/shard_map/reshape;reshape | solution.py:108
  507.4 20.2 %copy.81 = bf16[57344,128]{1,0:T(8,128)(2,1)} copy(bf16[57344,128]{0,1:T(8,128)(2,1)} %bitcast.238) | data formatting | bytes 29360128 | tf_op jit(solution)/shard_map/dot_general | solution.py:106
  527.6 35.5 %fusion.34 = f32[896,16,64]{0,1,2:T(8,128)} fusion(bf16[896,64,128]{2,1,0:T(8,128)(2,1)} %bitcast.237, s32[128]{0:T(128)S(1)} %eq.64), kind=kOutput, calls=%fused_computation.61 | convolution fusion | flops 234883072 | bytes 18350592 | tf_op jit(solution)/shard_map/dot_general | solution.py:106
  563.1 9.9 %add_reduce_fusion = (f32[16,64]{0,1:T(8,128)S(1)}, f32[448,16,64]{0,1,2:T(8,128)S(1)}, f32[448,16,64]{0,1,2:T(8,128)S(1)}) fusion(f32[448,16,64]{0,2,1:T(8,128)S(1)} %bitcast.241, f32[448,16,64]{0,2,1:T(8,128)} %bitcast.247, f32[448,16,64]{0,2,1:T(8,128)S(1)} %bitcast.243, f32[448,16,64]{0,2,1:T(8,128)S(1)} %bitcast.245, f32[16,64]{0,1:T(8,128)S(1)} %copy.87, ...), kind=kLoop, calls=%fused_computation.60 | loop fusion | flops 8256512 | bytes 14692352 | tf_op jit(solution)/shard_map/reduce_sum | solution.py:125
  575.6 1.7 fusion.19
  577.8 2.4 copy.96
  580.4 90.4 %psum.7 = f32[32]{0:T(128)} all-reduce(f32[32]{0:T(128)S(1)} %reduce_sum.51), channel_id=1, replica_groups=mesh['groups'=2,'sph'=16] {'sph'}, use_global_device_ids=true, to_apply=%region_8.9 | all-reduce | flops 32 | bytes 256 | tf_op jit(solution)/shard_map/psum | solution.py:126
  (184 shorter events, 67.9 us)
Async XLA Ops:
  0.6 15.6 %copy-start = (f32[2,448,256]{2,1,0:T(8,128)S(1)}, f32[2,448,256]{2,1,0:T(8,128)}, u32[]{:S(2)}) copy-start(f32[2,448,256]{2,1,0:T(8,128)} %param.14) | copy-start | bytes 2752516
  0.6 16.9 %copy-start.20 = (s32[64]{0:T(128)S(1)}, s32[64]{0:T(128)}, u32[]{:S(2)}) copy-start(s32[64]{0:T(128)} %param.19) | copy-start | bytes 772
  0.7 16.9 %copy-start.19 = (s32[64]{0:T(128)S(1)}, s32[64]{0:T(128)}, u32[]{:S(2)}) copy-start(s32[64]{0:T(128)} %param.21) | copy-start | bytes 772
  0.7 17.0 %copy-start.18 = (f32[2,448,32]{1,2,0:T(8,128)S(1)}, f32[2,448,32]{1,2,0:T(8,128)}, u32[]{:S(2)}) copy-start(f32[2,448,32]{1,2,0:T(8,128)} %param.16) | copy-start | bytes 344068
  5.5 181.1 %all-to-all-start = ((s32[16,1,8]{2,1,0:T(1,128)}), s32[16,1,8]{2,1,0:T(1,128)S(1)}, u32[]{:S(2)}, u32[]{:S(2)}) async-start(s32[16,1,8]{2,1,0:T(1,128)} %bitcast.24), calls=%async_computation | async-start | bytes 16384 | tf_op jit(solution)/shard_map/all_to_all | solution.py:99
  17.7 0.6 copy-start.12
  17.7 0.6 copy-start.14
  17.7 0.6 copy-start.10
  17.7 0.9 copy-start.16
  18.0 1.3 copy-start.3
  18.3 1.7 copy-start.5
  18.6 2.5 copy-start.7
  18.9 2.5 copy-start.9
  33.3 4.9 copy-start.2
  50.1 4.9 copy-start.2
  66.9 4.9 copy-start.2
  83.7 4.9 copy-start.2
  100.5 4.9 copy-start.2
  117.3 4.9 copy-start.2
  134.1 4.9 copy-start.2
  151.0 4.9 copy-start.2
  186.6 266.2 %all-to-all-start.1 = ((bf16[16,8,896,64]{2,3,1,0:T(8,128)(2,1)}), bf16[16,8,896,64]{2,3,1,0:T(8,128)(2,1)}, u32[]{:S(2)}, u32[]{:S(2)}) async-start(bf16[16,8,896,64]{2,3,1,0:T(8,128)(2,1)} %broadcast_multiply_fusion), calls=%async_computation.1 | async-start | bytes 29360128 | tf_op jit(solution)/shard_map/all_to_all | solution.py:98
  527.6 35.5 %copy-start.4 = (f32[448,32,32]{0,2,1:T(8,128)S(1)}, f32[448,32,32]{0,2,1:T(8,128)}, u32[]{:S(2)}) copy-start(f32[448,32,32]{0,2,1:T(8,128)} %copy-done.3) | copy-start | bytes 5505028
  527.6 35.5 %copy-start.6 = (f32[448,32,32]{0,2,1:T(8,128)S(1)}, f32[448,32,32]{0,2,1:T(8,128)}, u32[]{:S(2)}) copy-start(f32[448,32,32]{0,2,1:T(8,128)} %copy-done.5) | copy-start | bytes 5505028
  527.6 35.5 %copy-start.8 = (f32[448,32,32]{0,2,1:T(8,128)S(1)}, f32[448,32,32]{0,2,1:T(8,128)}, u32[]{:S(2)}) copy-start(f32[448,32,32]{0,2,1:T(8,128)} %copy-done.7) | copy-start | bytes 5505028
  574.2 1.3 copy-start.11
  574.3 1.3 copy-start.13
  574.3 1.3 copy-start.15
  574.3 1.3 copy-start.17
  577.2 93.6 %copy-start.1 = (f32[2,448,256]{2,1,0:T(8,128)S(1)}, f32[2,448,256]{2,1,0:T(8,128)}, u32[]{:S(2)}) copy-start(f32[2,448,256]{2,1,0:T(8,128)} %param.14) | copy-start | bytes 2752516
where the time goes:
time: 683 us; the launch traced here: 671 us
  waiting for transfers between devices  258 us (38%)
  local copies, waits for them, and re-layouts  172 us (25%)
  matrix products  94.1 us (14%)
  blocking collectives  90.4 us (13%)
  other arithmetic  41 us (6%)
  starting transfers between devices  13.5 us (2%)
    all_to_all x1, waiting for transfers between devices, shards(): lax.all_to_all(outgoing, 'sph', split_axis=0, concat_axis=0, tiled=True)  258 us
    psum x1, blocking collectives, shards(): extinction = lax.psum(local_ext, 'sph')  90.4 us
    gather x8, local copies, waits for them, and re-layouts, one_group(): tables = trans_table[picked]  56.2 us
    dot_general x1, matrix products, shards(): jnp.dot(gather_matrix, partial_value.reshape(slot_count, 2 * mode_count *...  35.5 us
    another operation x1, local copies, waits for them, and re-layouts, shards(): partial_value.reshape(slot_count, 2 * mode_count * columns)  28.1 us
    dot_general x8, matrix products, one_group(): jnp.einsum('kij,kjc->kic', tables[:, 0], data_real, preferred_element_typ...  27.6 us
    all_to_all x1, local copies, waits for them, and re-layouts, shards(): lax.all_to_all(outgoing, 'sph', split_axis=0, concat_axis=0, tiled=True)  26.5 us
    dot_general x1, local copies, waits for them, and re-layouts, shards(): jnp.dot(gather_matrix, partial_value.reshape(slot_count, 2 * mode_count *...  20.2 us
  transfers between devices with their start and end apart: 2, of which 1 were waited for; matrix products, arithmetic and copies ran while one was open for 26% of the time, Pallas kernels for 0%

commit v1 on v0

v1 whole, which is shorter than its diff:
```python
import jax
import jax.numpy as jnp
from jax import lax
from jax.experimental import pallas as pl
from jax.experimental.pallas import tpu as pltpu
from jax.sharding import PartitionSpec as P

BLOCK = 2
LANES = 128

HIGHEST_PRECISION = lax.Precision.HIGHEST


def field_kernel(
    starts,
    sources,
    own,
    cos_ref,
    sin_ref,
    pat_ref,
    mie_ref,
    table_ref,
    out_ref,
    ext_ref,
    sum_real,
    sum_imag,
    in_real,
    in_imag,
    in_neg,
    acc_real,
    acc_imag,
):
    step = pl.program_id(0)
    steps = pl.num_programs(0)
    dirs, modes = pat_ref.shape[1], pat_ref.shape[2]
    cols = BLOCK * dirs
    blocks = in_real.shape[0] // cols

    def phase_of(block):
        sphere = block * BLOCK
        tile = sphere // LANES
        shift = (LANES - sphere % LANES) % LANES
        return pltpu.roll(cos_ref[tile], shift, 1), pltpu.roll(sin_ref[tile], shift, 1)

    def incident(cosine, sine, j):
        c = cosine[:, j : j + 1]
        s = sine[:, j : j + 1]
        pr, pi = pat_ref[0], pat_ref[1]
        return c * pr - s * pi, c * pi + s * pr

    def mie_rows(block, j):
        sphere = block * BLOCK + j
        return mie_ref[0, pl.ds(sphere, 1), :], mie_ref[1, pl.ds(sphere, 1), :]

    def add_pair(q, first):
        block = sources[q]
        cosine, sine = phase_of(block)
        for j in range(BLOCK):
            ir, ii = incident(cosine, sine, j)
            mr, mi = mie_rows(block, j)
            rows = pl.ds(j * dirs, dirs)
            xr = mr * ir - mi * ii
            xi = mr * ii + mi * ir
            if first:
                sum_real[rows, :] = xr
                sum_imag[rows, :] = xi
            else:
                sum_real[rows, :] += xr
                sum_imag[rows, :] += xi

    def build(t, carry):
        low = starts[step * blocks + t]
        high = starts[step * blocks + t + 1]
        rows = pl.ds(pl.multiple_of(t * cols, cols), cols)

        @pl.when(high == low)
        def _():
            zero = jnp.zeros((cols, modes), jnp.bfloat16)
            in_real[rows, :] = zero
            in_imag[rows, :] = zero
            in_neg[rows, :] = zero

        @pl.when(high > low)
        def _():
            add_pair(low, True)

            def more(q, c):
                add_pair(q, False)
                return c

            lax.fori_loop(low + 1, high, more, 0)
            in_real[rows, :] = sum_real[...].astype(jnp.bfloat16)
            rounded = sum_imag[...].astype(jnp.bfloat16)
            in_imag[rows, :] = rounded
            in_neg[rows, :] = -rounded

        return carry

    lax.fori_loop(0, blocks, build, 0)

    def dot(a, b):
        return lax.dot_general(
            a, b, (((1,), (1,)), ((), ())), preferred_element_type=jnp.float32
        )

    table_real = table_ref[0, 0]
    table_imag = table_ref[0, 1]
    add_real = dot(in_real[...], table_real) + dot(in_neg[...], table_imag)
    add_imag = dot(in_real[...], table_imag) + dot(in_imag[...], table_real)

    @pl.when(step == 0)
    def _():
        acc_real[...] = add_real
        acc_imag[...] = add_imag

    @pl.when(step > 0)
    def _():
        acc_real[...] += add_real
        acc_imag[...] += add_imag

    @pl.when(step == steps - 1)
    def _():
        ext_ref[...] = jnp.zeros(ext_ref.shape, jnp.float32)
        per_tile = LANES // cols

        for tile in range(blocks // per_tile):
            real_rows, imag_rows = [], []
            for b in range(per_tile):
                local = tile * per_tile + b
                block = own[0] * blocks + local
                cosine, sine = phase_of(block)
                for j in range(BLOCK):
                    ir, ii = incident(cosine, sine, j)
                    mr, mi = mie_rows(block, j)
                    rows = pl.ds(local * cols + j * dirs, dirs)
                    tr = ir + acc_real[rows, :]
                    ti = ii + acc_imag[rows, :]
                    outr = mr * tr - mi * ti
                    outi = mr * ti + mi * tr
                    ext_ref[...] += ir * outr + ii * outi
                    real_rows.append(outr)
                    imag_rows.append(outi)
            at = pl.ds(tile * LANES, LANES)
            out_ref[0:modes, at] = jnp.concatenate(real_rows, 0).T.astype(jnp.bfloat16)
            out_ref[modes:, at] = jnp.concatenate(imag_rows, 0).T.astype(jnp.bfloat16)


def shards(
    positions,
    wave_vectors,
    pattern,
    dir_index,
    mie,
    trans_table,
    pair_route,
    pair_source,
    pair_target,
    pair_class,
):
    modes = pattern.shape[1]
    spheres = positions.shape[0]
    dirs = dir_index.shape[0]
    table_rows = wave_vectors.shape[0]
    classes = trans_table.shape[0]
    cols = BLOCK * dirs
    blocks = spheres // BLOCK
    devices = lax.axis_size("sph")
    me = lax.axis_index("sph")
    pair_count = pair_source.shape[0]
    capacity = max(2, 2 * pair_count // devices)
    slots = devices * capacity
    all_spheres = devices * spheres
    all_pairs = devices * pair_count

    small = jnp.concatenate(
        [
            positions.T.reshape(-1),
            pair_route[:, 0].astype(jnp.float32),
            pair_source.astype(jnp.float32),
            (pair_class * blocks + pair_target).astype(jnp.float32),
        ]
    )
    small = lax.all_gather(small, "sph", axis=0)
    mie_rows = lax.all_gather(mie.transpose(0, 2, 1), "sph", axis=1, tiled=True)

    everywhere = small[:, : 3 * spheres].reshape(devices, 3, spheres)
    listed = small[:, 3 * spheres :].reshape(devices, 3, pair_count).astype(jnp.int32)
    route = listed[:, 0].reshape(-1)
    source = (listed[:, 1] + jnp.arange(devices, dtype=jnp.int32)[:, None] * blocks).reshape(-1)
    slot_key = listed[:, 2].reshape(-1)
    key_count = classes * blocks
    key = jnp.where(route == me, slot_key, key_count)
    starts = jnp.sum(
        (key[None, :] < jnp.arange(key_count + 1, dtype=jnp.int32)[:, None]).astype(jnp.int32), 1
    )
    unique = key * all_pairs + jnp.arange(all_pairs, dtype=jnp.int32)
    place = jnp.sum((unique[None, :] < unique[:, None]).astype(jnp.int32), 1)
    sources = jnp.sum(
        jnp.where(place[None, :] == jnp.arange(slots, dtype=jnp.int32)[:, None], source[None, :], 0),
        1,
    )

    select = (jnp.arange(table_rows, dtype=jnp.int32)[:, None] == dir_index[None, :]).astype(
        jnp.float32
    )
    directions = jnp.dot(select.T, wave_vectors, precision=HIGHEST_PRECISION)
    chosen = jnp.einsum("cmt,td->cdm", pattern, select, precision=HIGHEST_PRECISION)
    tiles = -(-all_spheres // LANES)
    place3 = everywhere.transpose(1, 0, 2).reshape(3, all_spheres)
    place3 = jnp.pad(place3, ((0, 0), (0, tiles * LANES - all_spheres))).reshape(
        3, tiles, 1, LANES
    )
    phases = (
        place3[0] * directions[None, :, 0:1]
        + place3[1] * directions[None, :, 1:2]
        + place3[2] * directions[None, :, 2:3]
    )
    cosine = jnp.cos(phases)
    sine = jnp.sin(phases)

    whole = lambda *shape: pl.BlockSpec(shape, lambda c, *_: (0,) * len(shape))
    scattered, terms = pl.pallas_call(
        field_kernel,
        grid_spec=pltpu.PrefetchScalarGridSpec(
            num_scalar_prefetch=3,
            grid=(classes,),
            in_specs=[
                whole(*cosine.shape),
                whole(*sine.shape),
                whole(2, dirs, modes),
                whole(2, all_spheres, modes),
                pl.BlockSpec((1, 2, modes, modes), lambda c, *_: (c, 0, 0, 0)),
            ],
            out_specs=[whole(2 * modes, spheres * dirs), whole(dirs, modes)],
            scratch_shapes=[
                pltpu.VMEM((cols, modes), jnp.float32),
                pltpu.VMEM((cols, modes), jnp.float32),
                pltpu.VMEM((blocks * cols, modes), jnp.bfloat16),
                pltpu.VMEM((blocks * cols, modes), jnp.bfloat16),
                pltpu.VMEM((blocks * cols, modes), jnp.bfloat16),
                pltpu.VMEM((blocks * cols, modes), jnp.float32),
                pltpu.VMEM((blocks * cols, modes), jnp.float32),
            ],
        ),
        out_shape=[
            jax.ShapeDtypeStruct((2 * modes, spheres * dirs), jnp.bfloat16),
            jax.ShapeDtypeStruct((dirs, modes), jnp.float32),
        ],
        compiler_params=pltpu.CompilerParams(
            dimension_semantics=("arbitrary",), vmem_limit_bytes=56 * 1024 * 1024
        ),
    )(
        starts,
        sources,
        jnp.full((1,), me, jnp.int32),
        cosine,
        sine,
        chosen,
        mie_rows,
        trans_table,
    )
    extinction = lax.psum(jnp.sum(terms, axis=1), "sph")
    return (scattered, extinction)


def solution(mesh):
    placed = (
        P("sph", None),
        P(),
        P(),
        P("groups"),
        P(None, None, "sph"),
        P(),
        P("sph", None),
        P("sph"),
        P("sph"),
        P("sph"),
    )
    return jax.shard_map(
        shards,
        mesh=mesh,
        in_specs=placed,
        out_specs=(P(None, ("groups", "sph")), P("groups")),
        check_vma=False,
    )
```

time: 683 us -> 177 us (0.26); the launches traced: 671 us -> 179 us
  waiting for transfers between devices: 258 us -> 0.68 us
  local copies, waits for them, and re-layouts: 172 us -> 2.85 us
  matrix products: 94.1 us -> 2.77 us
  Pallas kernels: 0 us -> 41.9 us
  other arithmetic: 41 us -> 6.18 us
  blocking collectives: 90.4 us -> 110 us
  starting transfers between devices: 13.5 us -> 0.04 us
  between operations: 1.47 us -> 14.7 us
    all_to_all x2 -> x0, waiting for transfers between devices: 258 us -> none  [the longest x1 258 us: shards(): lax.all_to_all(outgoing, 'sph', split_axis=0, concat_axis=0, tiled=True)]
    dot_general x35 -> x2, matrix products: 94.1 us -> 2.77 us  [the longest x1 1.88 us: shards(): jnp.einsum('cmt,td->cdm', pattern, select, precision=HIGHEST_PRECISION)]
    gather x11 -> x0, local copies, waits for them, and re-layouts: 74.3 us -> none  [the longest x8 56.2 us: one_group(): tables = trans_table[picked]]
    unnamed x0 -> x1, blocking collectives: none -> 63.3 us
    psum x1, blocking collectives: 90.4 us -> 46.7 us  [shards(): extinction = lax.psum(jnp.sum(terms, axis=1), 'sph')]
    pallas_call x0 -> x1, Pallas kernels: none -> 41.9 us  [shards(): pl.pallas_call(field_kernel, grid_spec=pltpu.PrefetchScalarGridSpec(num_s...]
    another operation x1 -> x0, local copies, waits for them, and re-layouts: 28.1 us -> none  [shards(): partial_value.reshape(slot_count, 2 * mode_count * columns)]
    all_to_all x2 -> x0, local copies, waits for them, and re-layouts: 27 us -> none  [the longest x1 26.5 us: shards(): lax.all_to_all(outgoing, 'sph', split_axis=0, concat_axis=0, tiled=True)]
  transfers between devices with their start and end apart: 2 -> 1, of which waited for: 1 -> 0; matrix products, arithmetic and copies ran while one was open for 26% -> 6% of each run, Pallas kernels for 0% -> 0%
where the time goes in v1:
time: 177 us; the launch traced here: 179 us
  blocking collectives  110 us (62%)
  Pallas kernels  41.9 us (24%)
  between operations  14.7 us (8%)
  other arithmetic  6.18 us (3%)
  local copies, waits for them, and re-layouts  2.85 us (2%)
  matrix products  2.77 us (2%)
    unnamed x1, blocking collectives  63.3 us
    psum x1, blocking collectives, shards(): extinction = lax.psum(jnp.sum(terms, axis=1), 'sph')  46.7 us
    pallas_call x1, Pallas kernels, shards(): pl.pallas_call(field_kernel, grid_spec=pltpu.PrefetchScalarGridSpec(num_s...  41.9 us
  transfers between devices with their start and end apart: 1, of which 0 were waited for; matrix products, arithmetic and copies ran while one was open for 6% of the time, Pallas kernels for 0%

profile of v1, /device:TPU:0, one launch (start us, length us, event | category | flops | bytes accessed | tf_op | source)
XLA Modules:
  0.0 179.1 jit_solution(7101390082485535433)
XLA Ops:
  7.2 0.0 copy-start
  7.2 0.0 all-gather.3.cloned.1.call-start
  7.2 0.7 all-gather.3.cloned.1.call-update
  7.9 0.8 reshape.86
  8.7 0.7 convert_element_type.27
  9.3 0.1 add.38
  9.4 0.1 add.39
  9.5 1.2 dynamic-slice
  11.4 0.7 convert_bitcast_fusion
  12.0 0.7 add_convert_fusion
  12.7 0.2 maximum_dynamic-update-slice_fusion
  12.9 63.3 %all-reduce = f32[4608]{0:T(1024)S(1)} all-reduce(f32[4608]{0:T(1024)S(1)} %maximum_dynamic-update-slice_fusion), channel_id=2, replica_groups=mesh['groups'=2,'sph'=16] {'sph'}, use_global_device_ids=true, to_apply=%add | all-reduce | flops 4608 | bytes 36864
  76.2 0.1 reshape.88
  76.3 0.1 slice_convert_fusion
  76.3 0.1 convert_element_type.30
  76.4 0.1 slice_reduce_fusion.3
  76.5 0.1 squeeze.2
  76.5 0.1 select_n.23
  76.6 0.1 reshape.87
  76.7 0.1 slice_reduce_fusion.2
  76.8 0.1 mul.84
  76.8 0.1 mul.94
  76.9 0.1 mul.89
  77.0 0.7 convert_reduce_fusion.1.starts
  77.7 0.6 convert_reduce_fusion
  78.3 0.7 select_reduce_fusion.sources
  79.0 0.9 fusion.3
  79.8 1.0 fusion
  80.8 1.9 %convolution_bitcast_fusion.pat_ref = f32[2,32,448]{2,1,0:T(8,128)} fusion(f32[2,448,256]{2,1,0:T(8,128)S(1)} %copy-done, s32[32]{0:T(128)} %param.13), kind=kOutput, calls=%fused_computation.1 | convolution fusion | flops 88088576 | bytes 1032320 | tf_op jit(solution)/shard_map/cmt,td->cdm/dot_general | solution.py:207
  82.7 41.9 %shard_map.113 = (bf16[896,1024]{1,0:T(8,128)(2,1)}, f32[32,448]{1,0:T(8,128)}) custom-call(s32[129]{0:T(256)} %convert_reduce_fusion.1.starts, s32[128]{0:T(128)} %select_reduce_fusion.sources, s32[1]{0:T(128)} %bitcast.3.own, f32[4,32,128]{2,1,0:T(8,128)} %get-tuple-element.12.cos_ref, f32[4,32,128]{2,1,0:T(8,128)} %get-tuple-element.11.sin_ref, ...), custom_call_target="tpu_custom_call" | custom-call | tf_op jit(solution)/shard_map/pallas_call | solution.py:222
  124.6 1.0 reduce_sum.39
  125.6 46.7 %psum.7 = f32[32]{0:T(128)} all-reduce(f32[32]{0:T(128)S(1)} %reduce_sum.39), channel_id=1, replica_groups=mesh['groups'=2,'sph'=16] {'sph'}, use_global_device_ids=true, to_apply=%region_4.5 | all-reduce | flops 32 | bytes 256 | tf_op jit(solution)/shard_map/psum | solution.py:262
  (8 shorter events, 0.0 us)
Async XLA Ops:
  7.2 73.7 %copy-start = (f32[2,448,256]{2,1,0:T(8,128)S(1)}, f32[2,448,256]{2,1,0:T(8,128)}, u32[]{:S(2)}) copy-start(f32[2,448,256]{2,1,0:T(8,128)} %param.12) | copy-start | bytes 2752516
  7.2 75.5 %all-gather.3.cloned.1.call-start = ((), (), s32[]{:S(2)}) async-start(), calls=%async_computation | async-start | bytes 2228224 | tf_op jit(solution)/shard_map/all_gather | solution.py:184
Sparse Core Ops, SparseCore 0:
  10.2 44.4 all-gather.2

commit v2 on v1

--- a/solution.py
+++ b/solution.py
@@ -143,6 +143,13 @@
             at = pl.ds(tile * LANES, LANES)
             out_ref[0:modes, at] = jnp.concatenate(real_rows, 0).T.astype(jnp.bfloat16)
             out_ref[modes:, at] = jnp.concatenate(imag_rows, 0).T.astype(jnp.bfloat16)
+
+
+def exact_parts(x):
+    first = lax.reduce_precision(x, 8, 7)
+    second = lax.reduce_precision(x - first, 8, 7)
+    third = (x - first) - second
+    return jnp.stack([first, second, third])
 
 
 def shards(
@@ -172,22 +179,34 @@
     all_spheres = devices * spheres
     all_pairs = devices * pair_count
 
+    own_mie = mie.transpose(0, 2, 1)
+    rows = own_mie.astype(jnp.bfloat16).reshape(-1, LANES)
+    cut = rows.shape[0]
     small = jnp.concatenate(
         [
-            positions.T.reshape(-1),
+            exact_parts(positions.T.reshape(-1)).reshape(-1),
             pair_route[:, 0].astype(jnp.float32),
             pair_source.astype(jnp.float32),
-            (pair_class * blocks + pair_target).astype(jnp.float32),
+            pair_target.astype(jnp.float32),
+            pair_class.astype(jnp.float32),
         ]
     )
-    small = lax.all_gather(small, "sph", axis=0)
-    mie_rows = lax.all_gather(mie.transpose(0, 2, 1), "sph", axis=1, tiled=True)
-
-    everywhere = small[:, : 3 * spheres].reshape(devices, 3, spheres)
-    listed = small[:, 3 * spheres :].reshape(devices, 3, pair_count).astype(jnp.int32)
+    size = small.shape[0]
+    small = jnp.pad(small, (0, -size % (16 * LANES))).reshape(-1, LANES)
+    gathered = lax.all_gather(rows, "sph", axis=0)
+    tail = lax.all_to_all(
+        jnp.broadcast_to(small[None], (devices,) + small.shape), "sph", 0, 0, tiled=True
+    ).reshape(devices, -1)
+    mie_rows = gathered[:, :cut].reshape(devices, 2, spheres, modes).astype(jnp.float32)
+    mie_rows = mie_rows.transpose(1, 0, 2, 3).reshape(2, all_spheres, modes)
+    mie_rows = lax.dynamic_update_slice(mie_rows, own_mie, (0, me * spheres, 0))
+    split = 9 * spheres
+    pieces = tail[:, :split].reshape(devices, 3, 3, spheres)
+    everywhere = (pieces[:, 2] + pieces[:, 1]) + pieces[:, 0]
+    listed = tail[:, split:size].reshape(devices, 4, pair_count).astype(jnp.int32)
     route = listed[:, 0].reshape(-1)
     source = (listed[:, 1] + jnp.arange(devices, dtype=jnp.int32)[:, None] * blocks).reshape(-1)
-    slot_key = listed[:, 2].reshape(-1)
+    slot_key = (listed[:, 3] * blocks + listed[:, 2]).reshape(-1)
     key_count = classes * blocks
     key = jnp.where(route == me, slot_key, key_count)
     starts = jnp.sum(
@@ -259,7 +278,10 @@
         mie_rows,
         trans_table,
     )
-    extinction = lax.psum(jnp.sum(terms, axis=1), "sph")
+    local_terms = jnp.broadcast_to(jnp.sum(terms, axis=1)[None], (devices, dirs))
+    extinction = jnp.sum(
+        lax.all_to_all(local_terms, "sph", split_axis=0, concat_axis=0, tiled=True), axis=0
+    )
     return (scattered, extinction)
 
 

time: 177 us -> 117 us (0.66); the launches traced: 179 us -> 116 us
  blocking collectives: 110 us -> 34.6 us
  Pallas kernels: 41.9 us -> 56 us
  between operations: 14.7 us -> 0.75 us
  starting transfers between devices: 0.04 us -> 7.41 us
  local copies, waits for them, and re-layouts: 2.85 us -> 6.76 us
  other arithmetic: 6.18 us -> 8.13 us
    unnamed x1 -> x0, blocking collectives: 63.3 us -> none
    psum x1 -> x0, blocking collectives: 46.7 us -> none  [shards(): extinction = lax.psum(jnp.sum(terms, axis=1), 'sph')]
    all_gather x0 -> x1, blocking collectives: none -> 25.6 us  [shards(): gathered = lax.all_gather(rows, 'sph', axis=0)]
    pallas_call x1, Pallas kernels: 41.9 us -> 56 us  [shards(): pl.pallas_call(field_kernel, grid_spec=pltpu.PrefetchScalarGridSpec(num_s...]
    all_to_all x0 -> x1, blocking collectives: none -> 9.01 us  [shards(): lax.all_to_all(local_terms, 'sph', split_axis=0, concat_axis=0, tiled=True)]
    all_to_all x0 -> x1, starting transfers between devices: none -> 7.41 us  [shards(): lax.all_to_all(jnp.broadcast_to(small[None], (devices,) + small.shape), '...]
    reshape x1 -> x4, local copies, waits for them, and re-layouts: 0.08 us -> 3.61 us  [the longest x2 3.43 us: shards(): mie_rows = mie_rows.transpose(1, 0, 2, 3).reshape(2, all_spheres, modes)]
where the time goes in v2:
time: 117 us; the launch traced here: 116 us
  Pallas kernels  56 us (48%)
  blocking collectives  34.6 us (30%)
  other arithmetic  8.13 us (7%)
  starting transfers between devices  7.41 us (6%)
  local copies, waits for them, and re-layouts  6.76 us (6%)
  matrix products  2.11 us (2%)
    pallas_call x1, Pallas kernels, shards(): pl.pallas_call(field_kernel, grid_spec=pltpu.PrefetchScalarGridSpec(num_s...  56 us
    all_gather x1, blocking collectives, shards(): gathered = lax.all_gather(rows, 'sph', axis=0)  25.6 us
    all_to_all x1, blocking collectives, shards(): lax.all_to_all(local_terms, 'sph', split_axis=0, concat_axis=0, tiled=True)  9.01 us
    all_to_all x1, starting transfers between devices, shards(): lax.all_to_all(jnp.broadcast_to(small[None], (devices,) + small.shape), '...  7.41 us
    reshape x2, local copies, waits for them, and re-layouts, shards(): mie_rows = mie_rows.transpose(1, 0, 2, 3).reshape(2, all_spheres, modes)  3.43 us
  transfers between devices with their start and end apart: 1, of which 0 were waited for; matrix products, arithmetic and copies ran while one was open for 6% of the time, Pallas kernels for 0%

profile of v2, /device:TPU:0, one launch (start us, length us, event | category | flops | bytes accessed | tf_op | source)
XLA Modules:
  0.0 115.8 jit_solution(16241029069191112812)
XLA Ops:
  0.6 0.8 reshape.167
  1.5 0.1 reshape.168
  1.6 0.7 convert_bitcast_fusion
  2.3 0.7 convert_element_type.39
  2.9 0.7 convert_element_type.40
  3.6 0.7 convert_element_type.41
  4.2 0.1 concatenate.3
  4.3 0.7 broadcast_in_dim.25
  5.0 7.4 %all-to-all-start = ((f32[16,16,128]{2,1,0:T(8,128)}), f32[16,16,128]{2,1,0:T(8,128)S(1)}, u32[]{:S(2)}, u32[]{:S(2)}) async-start(f32[16,16,128]{2,1,0:T(8,128)} %broadcast_in_dim.25), calls=%async_computation | async-start | bytes 262144 | tf_op jit(solution)/shard_map/all_to_all | solution.py:197
  12.4 0.9 fusion.4
  13.3 0.1 add.64
  13.5 0.9 bitcast_convert_fusion
  14.4 0.1 all_gather_reshape.3
  14.5 25.6 %all_gather.3 = bf16[16,224,128]{2,1,0:T(8,128)(2,1)} all-gather(bf16[1,224,128]{2,1,0:T(8,128)(2,1)S(1)} %all_gather_reshape.3), channel_id=1, replica_groups=mesh['groups'=2,'sph'=16] {'sph'}, dimensions={0}, use_global_device_ids=true | all-gather | bytes 974848 | tf_op jit(solution)/shard_map/all_gather | solution.py:196
  40.2 1.9 %reshape.177 = f32[16,2,32,448]{3,2,1,0:T(8,128)S(1)} reshape(bf16[16,224,128]{2,1,0:T(8,128)(2,1)} %all_gather.3) | data formatting | bytes 2752512 | tf_op jit(solution)/shard_map/reshape | solution.py:201
  42.1 1.6 %copy.16 = f32[16,2,32,448]{3,2,0,1:T(8,128)} copy(f32[16,2,32,448]{3,2,1,0:T(8,128)S(1)} %reshape.177) | data formatting | bytes 3670016 | tf_op jit(solution)/shard_map/reshape | solution.py:201
  43.6 0.6 bitcast_dynamic-update-slice_fusion.mie_ref
  44.3 1.2 %convolution_bitcast_fusion.pat_ref = f32[2,32,448]{2,1,0:T(8,128)} fusion(f32[2,448,256]{2,1,0:T(8,128)S(1)} %copy-done, s32[32]{0:T(128)S(1)} %copy-done.2), kind=kOutput, calls=%fused_computation.1 | convolution fusion | flops 88088576 | bytes 1032320 | tf_op jit(solution)/shard_map/cmt,td->cdm/dot_general | solution.py:226
  45.6 0.1 slice_convert_fusion
  45.6 0.1 convert_element_type.43
  45.9 0.7 convert_reduce_fusion.1.starts
  46.6 0.1 reshape.170
  46.8 0.1 mul.100
  46.9 0.1 mul.105
  47.0 0.1 mul.110
  47.0 0.6 convert_reduce_fusion
  47.7 0.6 select_reduce_fusion.sources
  48.3 1.0 fusion
  49.3 56.0 %shard_map.113 = (bf16[896,1024]{1,0:T(8,128)(2,1)}, f32[32,448]{1,0:T(8,128)}) custom-call(s32[129]{0:T(256)} %convert_reduce_fusion.1.starts, s32[128]{0:T(128)} %select_reduce_fusion.sources, s32[1]{0:T(128)} %bitcast.3.own, f32[4,32,128]{2,1,0:T(8,128)} %get-tuple-element.12.cos_ref, f32[4,32,128]{2,1,0:T(8,128)} %get-tuple-element.11.sin_ref, ...), custom_call_target="tpu_custom_call" | custom-call | tf_op jit(solution)/shard_map/pallas_call | solution.py:241
  105.3 1.0 reduce_sum.48
  106.2 9.0 %all_to_all.11 = f32[16,1,32]{2,1,0:T(1,128)S(1)} all-to-all(f32[16,1,32]{2,1,0:T(1,128)S(1)} %broadcast_in_dim.50), channel_id=1, replica_groups=mesh['groups'=2,'sph'=16] {'sph'}, dimensions={0} | all-to-all | bytes 4096 | tf_op jit(solution)/shard_map/all_to_all | solution.py:283
  115.3 0.5 reduce_sum.49
  (23 shorter events, 0.5 us)
Async XLA Ops:
  0.6 43.6 %copy-start = (f32[2,448,256]{2,1,0:T(8,128)S(1)}, f32[2,448,256]{2,1,0:T(8,128)}, u32[]{:S(2)}) copy-start(f32[2,448,256]{2,1,0:T(8,128)} %param.12) | copy-start | bytes 2752516
  5.0 40.5 %all-to-all-start = ((f32[16,16,128]{2,1,0:T(8,128)}), f32[16,16,128]{2,1,0:T(8,128)S(1)}, u32[]{:S(2)}, u32[]{:S(2)}) async-start(f32[16,16,128]{2,1,0:T(8,128)} %broadcast_in_dim.25), calls=%async_computation | async-start | bytes 262144 | tf_op jit(solution)/shard_map/all_to_all | solution.py:197
  42.0 1.6 %copy-start.1 = (f32[2,448,32]{1,2,0:T(8,128)S(1)}, f32[2,448,32]{1,2,0:T(8,128)}, u32[]{:S(2)}) copy-start(f32[2,448,32]{1,2,0:T(8,128)} %param.14) | copy-start | bytes 344068
  42.0 2.2 %copy-start.2 = (s32[32]{0:T(128)S(1)}, s32[32]{0:T(128)}, u32[]{:S(2)}) copy-start(s32[32]{0:T(128)} %param.13) | copy-start | bytes 388
